TPU v7x, 128 devices: a whole 4x4x4 slice. The times are simulated.
128 devices in a mesh: replica: 1, data: 128 (over z, y, x, core).
Axes of the slice: x: 4, y: 4, z: 4, core: 2. Of those that a mesh axis runs over, the one named last changes fastest.
Arguments:
- query_hidden: bfloat16 [384, 32, 768], P(('replica', 'data'))
- doc_hidden: bfloat16 [384, 512, 768], P(('replica', 'data'))
- neg_hidden: bfloat16 [384, 4, 512, 768], P(('replica', 'data'))
- query_mask: int32 [384, 32], P(('replica', 'data'))
- doc_mask: int32 [384, 512], P(('replica', 'data'))
- neg_mask: int32 [384, 4, 512], P(('replica', 'data'))
- teacher: float32 [384, 5], P(('replica', 'data'))
- w_proj: bfloat16 [768, 128], replicated
- temperature: float32 [], replicated
Outputs:
- output 1: float32 [384], P(('replica', 'data'))
- output 2: float32 [1], P('replica')
All inputs are finite; a program needn't handle non-finite values.
Results may differ from a plain program's by a relative error of at most 0.001.
Values are sent between devices in bfloat16 or wider.
A program may use at most 1 GiB of HBM per device.

v0:
```python
import jax
import jax.numpy as jnp
from jax import lax
from jax.sharding import PartitionSpec as P


def project_tokens(hidden, w_proj):
    flat_hidden = hidden.reshape(-1, hidden.shape[-1])
    projected = jnp.dot(flat_hidden, w_proj, preferred_element_type=jnp.float32)
    projected = projected / jnp.sqrt(jnp.sum(projected * projected, axis=-1, keepdims=True))
    return projected.astype(jnp.bfloat16).reshape(hidden.shape[:-1] + (w_proj.shape[1],))


def hard_scores_of(query_tok, neg_tok, neg_mask):
    sim_tile = jnp.einsum('itd,iksd->itks', query_tok, neg_tok, preferred_element_type=jnp.float32)
    return jnp.sum(jnp.max(jnp.where(neg_mask[:, None] > 0, sim_tile, -jnp.inf), axis=3), axis=1)


def finish_loss(score_rows, positive, hard_scores, teacher, value_a11):
    logits = score_rows / value_a11
    pos_logit = positive / value_a11
    cross_ent = jax.nn.logsumexp(logits, axis=1) - pos_logit
    student = jnp.concatenate([pos_logit[:, None], hard_scores / value_a11], axis=1)
    student_log = jax.nn.log_softmax(student, axis=1)
    teacher_log = jax.nn.log_softmax(teacher, axis=1)
    return cross_ent + jnp.sum(jnp.exp(teacher_log) * (teacher_log - student_log), axis=1)


def solution(mesh):
    group_size = mesh.shape['data']
    batch_axes = ('replica', 'data')

    def local_loss(query_hidden, doc_hidden, neg_hidden, query_mask, doc_mask, neg_mask, teacher, w_proj, value_a11):
        local_batch = query_hidden.shape[0]
        query_tok = project_tokens(query_hidden, w_proj) * query_mask[:, :, None].astype(jnp.bfloat16)
        doc_tok = project_tokens(doc_hidden, w_proj)
        neg_tok = project_tokens(neg_hidden, w_proj)
        doc_valid = (doc_mask > 0)[None]
        query_steps = lax.all_gather(jnp.transpose(query_tok, (1, 0, 2)), 'data', axis=1, tiled=True)

        def token_step(running, query_step):
            sim_tile = jnp.einsum('id,jsd->ijs', query_step, doc_tok, preferred_element_type=jnp.float32)
            return running + jnp.max(jnp.where(doc_valid, sim_tile, -jnp.inf), axis=2), None

        start_cols = jnp.zeros((query_steps.shape[1], local_batch), jnp.float32)
        columns = lax.scan(token_step, start_cols, query_steps)[0]
        score_rows = lax.all_to_all(columns, 'data', 0, 1, tiled=True)
        my_index = lax.axis_index('data')
        own_block = lax.dynamic_slice_in_dim(score_rows, my_index * local_batch, local_batch, axis=1)
        hard_scores = hard_scores_of(query_tok, neg_tok, neg_mask)
        loss_rows = finish_loss(score_rows, jnp.diagonal(own_block), hard_scores, teacher, value_a11)
        loss_mean = lax.psum(jnp.sum(loss_rows), 'data') / (local_batch * group_size)
        return loss_rows, loss_mean.reshape(1)

    in_specs = (P(batch_axes, None, None), P(batch_axes, None, None), P(batch_axes, None, None, None),
                P(batch_axes, None), P(batch_axes, None), P(batch_axes, None, None), P(batch_axes, None),
                P(None, None), P())
    out_specs = (P(batch_axes), P('replica'))
    return jax.shard_map(local_loss, mesh=mesh, in_specs=in_specs, out_specs=out_specs, check_vma=False)
```

profile of v0, /device:TPU:1, one launch (start us, length us, event | category | flops | bytes accessed | tf_op | source)
XLA Modules:
  0.0 224.3 jit_solution(5742312536760787990)
XLA Ops:
  10.2 8.0 %multiply_reduce_fusion = (f32[6144]{0:T(1024)S(1)}, f32[6144,128]{1,0:T(8,128)}) fusion(bf16[6144,768]{1,0:T(8,128)(2,1)} %bitcast.47, bf16[768,128]{1,0:T(8,128)(2,1)} %param.19), kind=kOutput, calls=%fused_computation.7 | convolution fusion | flops 1209526272 | bytes 12804096 | tf_op jit(solution)/shard_map/dot_general | solution.py:9
  24.9 55.5 %all-gather.2.cloned.1.call-done = bf16[32,384,128]{2,0,1:T(8,128)(2,1)} async-done(((bf16[32,3,128]{2,0,1:T(8,128)(2,1)}), bf16[32,384,128]{2,0,1:T(8,128)(2,1)}) %all-gather.2.cloned.1.call-update) | async-done | bytes 3145744 | tf_op jit(solution)/shard_map/all_gather | solution.py:39
  80.4 4.8 %copy.20 = bf16[32,384,128]{2,1,0:T(8,128)(2,1)} copy(bf16[32,384,128]{2,0,1:T(8,128)(2,1)} %all-gather.2.cloned.1.call-done) | data formatting | bytes 6291456
  85.2 47.3 %while.11 = (s32[]{:T(128)}, f32[384,3]{0,1:T(4,128)S(1)}, pred[1,3,512]{2,1,0:T(4,128)(4,1)S(1)}, bf16[32,384,128]{2,1,0:T(8,128)(2,1)}, bf16[3,512,128]{2,1,0:T(8,128)(2,1)S(1)}, /*index=5*/s32[]{:T(128)}, s32[]{:T(128)}) while((s32[]{:T(128)}, f32[384,3]{0,1:T(4,128)S(1)}, pred[1,3,512]{2,1,0:T(4,128)(4,1)S(1)}, ...), condition=%wide.region_4.5_spmd.clone, body=%wide.region_2.4_spmd.clone.sunk | while | flops 152175744 | bytes 511587 | solution.py:46
  85.2 1.4 select_reduce_fusion.2
  86.7 1.4 select_reduce_fusion.2
  88.2 1.4 select_reduce_fusion.2
  89.7 1.4 select_reduce_fusion.2
  92.6 1.4 select_reduce_fusion.2
  94.1 1.4 select_reduce_fusion.2
  95.6 1.4 select_reduce_fusion.2
  97.1 1.4 select_reduce_fusion.2
  100.0 1.4 select_reduce_fusion.2
  101.5 1.4 select_reduce_fusion.2
  103.0 1.4 select_reduce_fusion.2
  104.5 1.4 select_reduce_fusion.2
  107.4 1.4 select_reduce_fusion.2
  108.9 1.4 select_reduce_fusion.2
  111.9 1.4 select_reduce_fusion.2
  114.8 1.4 select_reduce_fusion.2
  116.3 1.4 select_reduce_fusion.2
  117.8 1.4 select_reduce_fusion.2
  119.3 1.4 select_reduce_fusion.2
  122.2 1.4 select_reduce_fusion.2
  123.7 1.4 select_reduce_fusion.2
  125.2 1.4 select_reduce_fusion.2
  126.6 1.4 select_reduce_fusion.2
  129.6 1.4 select_reduce_fusion.2
  131.1 1.4 select_reduce_fusion.2
  133.6 5.3 %all-to-all-start = ((f32[128,3,3]{1,2,0:T(4,128)}), f32[128,3,3]{1,2,0:T(4,128)S(1)}, u32[]{:S(2)}, u32[]{:S(2)}) async-start(f32[128,3,3]{1,2,0:T(4,128)} %copy.21), calls=%async_computation | async-start | bytes 524288 | tf_op jit(solution)/shard_map/all_to_all | solution.py:47
  138.9 10.8 %all-to-all-done = f32[128,3,3]{1,2,0:T(4,128)S(1)} async-done(((f32[128,3,3]{1,2,0:T(4,128)}), f32[128,3,3]{1,2,0:T(4,128)S(1)}, u32[]{:S(2)}, u32[]{:S(2)}) %all-to-all-start) | async-done | bytes 4640 | tf_op jit(solution)/shard_map/all_to_all | solution.py:47
  152.8 62.8 %psum.7 = f32[]{:T(128)} all-reduce(f32[]{:T(128)} %get-tuple-element.64), channel_id=1, replica_groups=mesh['replica'=1,'data'=128] {'data'}, use_global_device_ids=true, to_apply=%region_14.16 | all-reduce | flops 1 | bytes 8 | tf_op jit(solution)/shard_map/psum | solution.py:52
  (101 shorter events, 23.5 us)
Async XLA Ops:
  7.2 11.7 %copy-start = (bf16[3,512,768]{2,1,0:T(8,128)(2,1)S(1)}, bf16[3,512,768]{2,1,0:T(8,128)(2,1)}, u32[]{:S(2)}) copy-start(bf16[3,512,768]{2,1,0:T(8,128)(2,1)} %param.13) | copy-start | bytes 7077892
  7.2 73.2 %all-gather.2.cloned.1.call-start = ((), (), s32[]{:S(2)}) async-start(), calls=%async_computation.1 | async-start | bytes 3170304 | tf_op jit(solution)/shard_map/all_gather | solution.py:39
  10.2 8.7 %copy-start.2 = (bf16[768,128]{1,0:T(8,128)(2,1)S(1)}, bf16[768,128]{1,0:T(8,128)(2,1)}, u32[]{:S(2)}) copy-start(bf16[768,128]{1,0:T(8,128)(2,1)} %param.19) | copy-start | bytes 589828
  18.2 1.6 copy-start.4
  18.9 1.9 copy-start.1
  20.8 1.8 copy-start.5
  20.8 3.3 %copy-start.7 = (s32[3,512]{1,0:T(4,128)S(1)}, s32[3,512]{1,0:T(4,128)}, u32[]{:S(2)}) copy-start(s32[3,512]{1,0:T(4,128)} %param.16) | copy-start | bytes 18436
  22.7 1.9 copy-start.8
  24.9 60.3 %copy-start.10 = (pred[1,3,512]{2,1,0:T(4,128)(4,1)S(1)}, pred[1,3,512]{2,1,0:T(4,128)(4,1)}, u32[]{:S(2)}) copy-start(pred[1,3,512]{2,1,0:T(4,128)(4,1)} %compare_bitcast_fusion) | copy-start | bytes 4612
  85.2 53.7 %copy-start.11 = (f32[3]{0:T(128)S(1)}, f32[3]{0:T(128)}, u32[]{:S(2)}) copy-start(f32[3]{0:T(128)} %exponential_reduce_fusion.2) | copy-start | bytes 40
  85.2 65.5 %copy-start.3 = (f32[3,4]{1,0:T(4,128)S(1)}, f32[3,4]{1,0:T(4,128)}, u32[]{:S(2)}) copy-start(f32[3,4]{1,0:T(4,128)} %broadcast_divide_fusion.1) | copy-start | bytes 148
  85.2 66.1 %copy-start.6 = (f32[3,5]{1,0:T(4,128)S(1)}, f32[3,5]{1,0:T(4,128)}, u32[]{:S(2)}) copy-start(f32[3,5]{1,0:T(4,128)} %param.18) | copy-start | bytes 184
  85.2 66.1 %copy-start.9 = (f32[3]{0:T(128)S(1)}, f32[3]{0:T(128)}, u32[]{:S(2)}) copy-start(f32[3]{0:T(128)} %copy-done.8) | copy-start | bytes 40
  133.6 16.2 %all-to-all-start = ((f32[128,3,3]{1,2,0:T(4,128)}), f32[128,3,3]{1,2,0:T(4,128)S(1)}, u32[]{:S(2)}, u32[]{:S(2)}) async-start(f32[128,3,3]{1,2,0:T(4,128)} %copy.21), calls=%async_computation | async-start | bytes 524288 | tf_op jit(solution)/shard_map/all_to_all | solution.py:47
Sparse Core Ops, SparseCore 0:
  11.1 69.2 all-gather.1
where the time goes:
time: 226 us; the launch traced here: 224 us
  waiting for transfers between devices  66.3 us (29%)
  blocking collectives  62.8 us (28%)
  matrix products  57.3 us (25%)
  between operations  16.7 us (7%)
  local copies, waits for them, and re-layouts  7.83 us (3%)
  other arithmetic  7.26 us (3%)
  starting transfers between devices  5.33 us (2%)
    psum x1, blocking collectives, local_loss(): lax.psum(jnp.sum(loss_rows), 'data') / (local_batch * group_size)  62.8 us
    all_gather x1, waiting for transfers between devices, local_loss(): lax.all_gather(jnp.transpose(query_tok, (1, 0, 2)), 'data', axis=1, tiled...  55.5 us
    dot_general x32, matrix products, token_step(): jnp.einsum('id,jsd->ijs', query_step, doc_tok, preferred_element_type=jnp...  46.2 us
    all_to_all x1, waiting for transfers between devices, local_loss(): score_rows = lax.all_to_all(columns, 'data', 0, 1, tiled=True)  10.8 us
    dot_general x3, matrix products, project_tokens(): projected = jnp.dot(flat_hidden, w_proj, preferred_element_type=jnp.float32)  10.3 us
    unnamed x26, local copies, waits for them, and re-layouts  5.91 us
    all_to_all x1, starting transfers between devices, local_loss(): score_rows = lax.all_to_all(columns, 'data', 0, 1, tiled=True)  5.3 us
  transfers between devices with their start and end apart: 2, of which 2 were waited for; matrix products, arithmetic and copies ran while one was open for 6% of the time, Pallas kernels for 0%

commit v1 on v0

v1 whole, which is shorter than its diff:
```python
import functools

import jax
import jax.numpy as jnp
from jax import lax
from jax.experimental import pallas as pl
from jax.experimental.pallas import tpu as pltpu
from jax.sharding import PartitionSpec as P

RING = 4
CHIPS = RING ** 3
PLANE = RING * RING
ORDERS = ((0, 1, 2), (1, 2, 0), (2, 0, 1))
UNITS = 16
LOW = -3.0e38


def kernel(qh, dh, nh, qm, dm, nm, te, w, tau_ref, loss_ref, mean_ref,
           qv, dv, nv, qmv, dmv, nmv, tev, wv, gath, docs, best, hard, part, inbox, tot, totin,
           in_sem, doc_sem, gsend, grecv, psend, precv, tsem):
    me = lax.axis_index('data')
    core = lax.rem(me, 2)
    chip = me // 2
    pos = (lax.rem(chip, RING), lax.rem(chip // RING, RING), chip // PLANE)
    nq, dlen = dv.shape[0], dv.shape[1]
    nneg = nv.shape[1]
    qlen = qv.shape[1]

    def device(axis, off):
        c = list(pos)
        c[axis] = lax.rem(pos[axis] + off, RING)
        return {'data': ((c[2] * RING + c[1]) * RING + c[0]) * 2 + core}

    partner = {'data': chip * 2 + 1 - core}

    loads = [pltpu.make_async_copy(w, wv, in_sem.at[0]),
             pltpu.make_async_copy(qh, qv, in_sem.at[1]),
             pltpu.make_async_copy(qm, qmv, in_sem.at[2]),
             pltpu.make_async_copy(dm, dmv, in_sem.at[3]),
             pltpu.make_async_copy(nm, nmv, in_sem.at[4]),
             pltpu.make_async_copy(te, tev, in_sem.at[5])]
    doc_loads = [pltpu.make_async_copy(dh.at[j], dv.at[j], in_sem.at[6 + j]) for j in range(nq)]
    neg_loads = [pltpu.make_async_copy(nh.at[i], nv.at[i], in_sem.at[6 + nq + i]) for i in range(nq)]
    for load in loads + doc_loads + neg_loads:
        load.start()

    barrier = pltpu.get_barrier_semaphore()
    for axis in range(3):
        for off in range(1, RING):
            pl.semaphore_signal(barrier, inc=1, device_id=device(axis, off), device_id_type=pl.DeviceIdType.MESH)
    pl.semaphore_signal(barrier, inc=1, device_id=partner, device_id_type=pl.DeviceIdType.MESH)

    def project(rows):
        y = jnp.dot(rows, wv[...], preferred_element_type=jnp.float32)
        return y * lax.rsqrt(jnp.sum(y * y, axis=-1, keepdims=True))

    def length(mask_row):
        return jnp.sum(mask_row.astype(jnp.float32), axis=-1, keepdims=True)

    def row_ids(rows, cols):
        return lax.broadcasted_iota(jnp.int32, (rows, cols), 0).astype(jnp.float32)

    hard[...] = jnp.zeros_like(hard)
    best[...] = jnp.zeros_like(best)
    for load in loads:
        load.wait()

    own = []
    for q in range(nq):
        a1, a2, a3 = ORDERS[q]
        own.append((pos[a3] * RING + pos[a2]) * RING + pos[a1])
        tok = project(qv[q])
        keep = row_ids(qlen, tok.shape[1]) < length(qmv[q:q + 1, :])
        gath[q, own[q]] = jnp.where(keep, tok, 0.0).astype(jnp.bfloat16)

    pl.semaphore_wait(barrier, 3 * (RING - 1) + 1)

    def copies(stage, q):
        axis = ORDERS[q][stage]
        span = RING ** stage
        a1, a2, a3 = ORDERS[q]
        out = []
        for off in range(1, RING):
            def start_of(shift):
                c = list(pos)
                c[axis] = lax.rem(pos[axis] + shift, RING)
                flat = (c[a3] * RING + c[a2]) * RING + c[a1]
                return flat if span == 1 else (flat // span) * span
            mine = gath.at[q, pl.ds(start_of(0), span)]
            theirs = gath.at[q, pl.ds(start_of(RING - off), span)]
            send = pltpu.make_async_remote_copy(
                src_ref=mine, dst_ref=mine, send_sem=gsend.at[stage, q, off - 1], recv_sem=grecv.at[stage, q, off - 1],
                device_id=device(axis, off), device_id_type=pl.DeviceIdType.MESH)
            recv = pltpu.make_async_remote_copy(
                src_ref=theirs, dst_ref=theirs, send_sem=gsend.at[stage, q, off - 1],
                recv_sem=grecv.at[stage, q, off - 1],
                device_id=device(axis, off), device_id_type=pl.DeviceIdType.MESH)
            out.append((send, recv))
        return out

    gather = [[copies(stage, q) for q in range(nq)] for stage in range(3)]

    for q in range(nq):
        for send, _ in gather[0][q]:
            send.start()

    def valid_rows(y, mask_row):
        keep = row_ids(dlen, y.shape[1]) < length(mask_row)
        return jnp.where(keep, y, y[0:1, :]).astype(jnp.bfloat16)

    for j in range(nq):
        doc_loads[j].wait()
        docs[core * nq + j] = valid_rows(project(dv[j]), dmv[j:j + 1, :])

    my_docs = docs.at[pl.ds(core * nq, nq)]
    their_docs = docs.at[pl.ds((1 - core) * nq, nq)]
    doc_send = pltpu.make_async_remote_copy(
        src_ref=my_docs, dst_ref=my_docs, send_sem=doc_sem.at[0], recv_sem=doc_sem.at[1],
        device_id=partner, device_id_type=pl.DeviceIdType.MESH)
    doc_recv = pltpu.make_async_remote_copy(
        src_ref=their_docs, dst_ref=their_docs, send_sem=doc_sem.at[0], recv_sem=doc_sem.at[1],
        device_id=partner, device_id_type=pl.DeviceIdType.MESH)
    contract = (((1,), (1,)), ((), ()))
    cell_row = lax.broadcasted_iota(jnp.int32, hard.shape, 0)
    cell_lane = lax.broadcasted_iota(jnp.int32, hard.shape, 1)

    def negatives(i):
        neg_loads[i].wait()
        mine = gath[i, own[i]]
        for k in range(nneg):
            tok = valid_rows(project(nv[i, k]), nmv[i, k:k + 1, :])
            sim = lax.dot_general(tok, mine, contract, preferred_element_type=jnp.float32)
            score = jnp.sum(jnp.max(sim, axis=0, keepdims=True), axis=1, keepdims=True)
            hard[...] = jnp.where((cell_row == i) & (cell_lane == k + 1), score, hard[...])

    def forward(stage):
        for q in range(nq):
            for _, recv in gather[stage - 1][q]:
                recv.wait_recv()
            for send, _ in gather[stage][q]:
                send.start()

    negatives(0)
    doc_send.start()
    forward(1)
    negatives(1)
    forward(2)
    negatives(2)
    doc_recv.wait_recv()

    unit_row = lax.broadcasted_iota(jnp.int32, (8, PLANE * qlen), 0)

    def score_unit(q, plane):
        rows = gath[q, pl.ds(plane * PLANE, PLANE)].reshape(PLANE * qlen, gath.shape[3])
        unit = jnp.zeros((8, PLANE * qlen), jnp.float32)
        for j in range(2 * nq):
            halves = []
            for h in range(PLANE * qlen // 256):
                sim = lax.dot_general(docs[j], rows[h * 256:(h + 1) * 256], contract,
                                      preferred_element_type=jnp.float32)
                halves.append(jnp.max(sim, axis=0, keepdims=True))
            unit = jnp.where(unit_row == j, jnp.concatenate(halves, axis=1), unit)
        best[q * RING + plane] = unit

    for q in range(nq):
        score_unit(q, pos[ORDERS[q][2]])
    for off in (1, 3, 2):
        for q in range(nq):
            gather[2][q][off - 1][1].wait_recv()
            score_unit(q, lax.rem(pos[ORDERS[q][2]] + RING - off, RING))

    tau = tau_ref[0]
    flat = best[...].reshape(UNITS * 8, PLANE * qlen)
    first = lax.broadcasted_iota(jnp.int32, (PLANE * qlen, 128), 1) * qlen
    token = lax.broadcasted_iota(jnp.int32, (PLANE * qlen, 128), 0)
    ones = jnp.where((token >= first) & (token < first + qlen), 1.0, 0.0)
    scores = lax.dot_general(flat, ones, (((1,), (0,)), ((), ())), precision=lax.Precision.HIGHEST,
                             preferred_element_type=jnp.float32).reshape(UNITS, 8, 128)
    u_id = lax.broadcasted_iota(jnp.int32, (UNITS, 8, 128), 0)
    j_id = lax.broadcasted_iota(jnp.int32, (UNITS, 8, 128), 1)
    l_id = lax.broadcasted_iota(jnp.int32, (UNITS, 8, 128), 2)

    students = hard[...]
    for q in range(nq):
        a1, a2, a3 = ORDERS[q]
        here = (u_id == q * RING + pos[a3]) & (j_id == core * nq + q) & (l_id == pos[a2] * RING + pos[a1])
        hit = jnp.sum(jnp.where(here, scores, 0.0), axis=0)
        hit = jnp.sum(jnp.sum(hit, axis=0, keepdims=True), axis=1, keepdims=True)
        students = jnp.where((cell_row == q) & (cell_lane == 0), hit, students)

    def log_softmax(z):
        z = z - jnp.max(z, axis=1, keepdims=True)
        return z - jnp.log(jnp.sum(jnp.exp(z), axis=1, keepdims=True))

    logits = students[:nq, :nneg + 1] / tau
    teacher_log = log_softmax(tev[...])
    student_log = log_softmax(logits)
    rest = jnp.sum(jnp.exp(teacher_log) * (teacher_log - student_log), axis=1, keepdims=True) - logits[:, 0:1]
    rest_sum = jnp.sum(rest, axis=0, keepdims=True)

    real = j_id < 2 * nq
    top = jnp.max(jnp.where(real, scores, LOW), axis=1, keepdims=True)
    mass = jnp.sum(jnp.where(real, jnp.exp((scores - top) / tau), 0.0), axis=1)
    top = top.reshape(UNITS, 128)
    p_row = lax.broadcasted_iota(jnp.int32, (UNITS, 128), 0)
    p_lane = lax.broadcasted_iota(jnp.int32, (UNITS, 128), 1)
    used = p_row < nq * RING
    mass = jnp.where(used, mass, jnp.where((p_row == nq * RING) & (p_lane == 0), rest_sum, 0.0))
    top = jnp.where(used, top, 0.0)

    for stage in range(3):
        part[stage, 0] = top
        part[stage, 1] = mass
        moves = []
        for off in range(1, RING):
            move = pltpu.make_async_remote_copy(
                src_ref=part.at[stage], dst_ref=inbox.at[stage, off - 1], send_sem=psend.at[stage, off - 1],
                recv_sem=precv.at[stage, off - 1], device_id=device(stage, off),
                device_id_type=pl.DeviceIdType.MESH)
            move.start()
            moves.append(move)
        for move in moves:
            move.wait()
        tops = [top] + [inbox[stage, o, 0] for o in range(RING - 1)]
        masses = [mass] + [inbox[stage, o, 1] for o in range(RING - 1)]
        top = functools.reduce(jnp.maximum, tops)
        mass = sum(ms * jnp.exp((tp - top) / tau) for tp, ms in zip(tops, masses))

    lse = jnp.where(used & (p_lane < PLANE), top / tau + jnp.log(jnp.where(used, mass, 1.0)), 0.0)
    extra = jnp.where((p_row == nq * RING) & (p_lane == 0), mass, 0.0)
    mine = jnp.sum(jnp.sum(lse + extra, axis=0, keepdims=True), axis=1, keepdims=True)
    tot[...] = jnp.broadcast_to(mine, tot.shape)
    swap = pltpu.make_async_remote_copy(
        src_ref=tot, dst_ref=totin, send_sem=tsem.at[0], recv_sem=tsem.at[1],
        device_id=partner, device_id_type=pl.DeviceIdType.MESH)
    swap.start()
    rest_row = lax.broadcasted_iota(jnp.int32, rest.shape, 0)
    for q in range(nq):
        a1, a2, a3 = ORDERS[q]
        here = (p_row == q * RING + pos[a3]) & (p_lane == pos[a2] * RING + pos[a1])
        loss_ref[q] = jnp.sum(jnp.where(here, lse, 0.0)) + jnp.sum(jnp.where(rest_row == q, rest, 0.0))
    swap.wait()
    mean_ref[0] = jnp.sum((tot[0:1, 0:1] + totin[0:1, 0:1]) / (2 * CHIPS * nq))

    doc_send.wait_send()
    for stage in range(3):
        for q in range(nq):
            for send, _ in gather[stage][q]:
                send.wait_send()


def solution(mesh):
    batch_axes = ('replica', 'data')

    def local_loss(query_hidden, doc_hidden, neg_hidden, query_mask, doc_mask, neg_mask, teacher, w_proj, temperature):
        nq, qlen, width = query_hidden.shape
        dlen, nneg = doc_hidden.shape[1], neg_hidden.shape[1]
        proj = w_proj.shape[1]
        anywhere = pl.BlockSpec(memory_space=pl.ANY)
        smem = pl.BlockSpec(memory_space=pltpu.SMEM)
        rows = nq * (qlen + dlen + nneg * dlen)
        loss, mean = pl.pallas_call(
            kernel,
            name='late_interaction',
            out_shape=(jax.ShapeDtypeStruct((nq,), jnp.float32), jax.ShapeDtypeStruct((1,), jnp.float32)),
            in_specs=[anywhere] * 8 + [smem],
            out_specs=(smem, smem),
            scratch_shapes=[
                pltpu.VMEM(query_hidden.shape, jnp.bfloat16),
                pltpu.VMEM(doc_hidden.shape, jnp.bfloat16),
                pltpu.VMEM(neg_hidden.shape, jnp.bfloat16),
                pltpu.VMEM(query_mask.shape, jnp.int32),
                pltpu.VMEM(doc_mask.shape, jnp.int32),
                pltpu.VMEM(neg_mask.shape, jnp.int32),
                pltpu.VMEM(teacher.shape, jnp.float32),
                pltpu.VMEM(w_proj.shape, jnp.bfloat16),
                pltpu.VMEM((nq, CHIPS, qlen, proj), jnp.bfloat16),
                pltpu.VMEM((2 * nq, dlen, proj), jnp.bfloat16),
                pltpu.VMEM((UNITS, 8, PLANE * qlen), jnp.float32),
                pltpu.VMEM((8, 128), jnp.float32),
                pltpu.VMEM((3, 2, UNITS, 128), jnp.float32),
                pltpu.VMEM((3, RING - 1, 2, UNITS, 128), jnp.float32),
                pltpu.VMEM((8, 128), jnp.float32),
                pltpu.VMEM((8, 128), jnp.float32),
                pltpu.SemaphoreType.DMA((6 + 2 * nq,)),
                pltpu.SemaphoreType.DMA((2,)),
                pltpu.SemaphoreType.DMA((3, nq, RING - 1)),
                pltpu.SemaphoreType.DMA((3, nq, RING - 1)),
                pltpu.SemaphoreType.DMA((3, RING - 1)),
                pltpu.SemaphoreType.DMA((3, RING - 1)),
                pltpu.SemaphoreType.DMA((2,)),
            ],
            compiler_params=pltpu.CompilerParams(
                collective_id=0, has_side_effects=True, vmem_limit_bytes=60 * 1024 * 1024),
            cost_estimate=pl.CostEstimate(
                flops=2 * proj * (rows * width + CHIPS * nq * qlen * 2 * nq * dlen),
                bytes_accessed=2 * rows * width, transcendentals=rows),
        )(query_hidden, doc_hidden, neg_hidden, query_mask, doc_mask, neg_mask, teacher, w_proj,
          temperature.reshape(1))
        return loss, mean

    in_specs = (P(batch_axes, None, None), P(batch_axes, None, None), P(batch_axes, None, None, None),
                P(batch_axes, None), P(batch_axes, None), P(batch_axes, None, None), P(batch_axes, None),
                P(None, None), P())
    out_specs = (P(batch_axes), P('replica'))
    return jax.shard_map(local_loss, mesh=mesh, in_specs=in_specs, out_specs=out_specs, check_vma=False)
```

time: 226 us -> 49.7 us (0.22)
  waiting for transfers between devices: 66.3 us -> 0 us
  blocking collectives: 62.8 us -> 0 us
  matrix products: 57.3 us -> 0 us
  Pallas kernels: 0 us -> 45.4 us
  between operations: 16.7 us -> 3.05 us
  other arithmetic: 7.26 us -> 0 us
  local copies, waits for them, and re-layouts: 7.83 us -> 1.11 us
  starting transfers between devices: 5.33 us -> 0 us
    psum x1 -> x0, blocking collectives: 62.8 us -> none  [local_loss(): lax.psum(jnp.sum(loss_rows), 'data') / (local_batch * group_size)]
    dot_general x36 -> x0, matrix products: 57.3 us -> none  [the longest x32 46.2 us: token_step(): jnp.einsum('id,jsd->ijs', query_step, doc_tok, preferred_element_type=jnp...]
    all_gather x1 -> x0, waiting for transfers between devices: 55.5 us -> none  [local_loss(): lax.all_gather(jnp.transpose(query_tok, (1, 0, 2)), 'data', axis=1, tiled...]
    pallas_call x0 -> x1, Pallas kernels: none -> 45.4 us  [local_loss(): pl.pallas_call(kernel, name='late_interaction', out_shape=(jax.ShapeDtype...]
    all_to_all x1 -> x0, waiting for transfers between devices: 10.8 us -> none  [local_loss(): score_rows = lax.all_to_all(columns, 'data', 0, 1, tiled=True)]
    all_to_all x1 -> x0, starting transfers between devices: 5.3 us -> none  [local_loss(): score_rows = lax.all_to_all(columns, 'data', 0, 1, tiled=True)]
    unnamed x26 -> x1, local copies, waits for them, and re-layouts: 5.91 us -> 1.11 us
    reduce_sum x6 -> x0, other arithmetic: 2.46 us -> none  [the longest x1 1.13 us: local_loss(): jnp.sum(loss_rows)]
  transfers between devices with their start and end apart: 2 -> 0, of which waited for: 2 -> 0; matrix products, arithmetic and copies ran while one was open for 6% -> 0% of each run, Pallas kernels for 0% -> 0%
where the time goes in v1:
time: 49.7 us; the launch traced here: 49.5 us
  Pallas kernels  45.4 us (91%)
  between operations  3.05 us (6%)
  local copies, waits for them, and re-layouts  1.11 us (2%)
    pallas_call x1, Pallas kernels, local_loss(): pl.pallas_call(kernel, name='late_interaction', out_shape=(jax.ShapeDtype...  45.4 us
    unnamed x1, local copies, waits for them, and re-layouts  1.11 us

profile of v1, /device:TPU:1, one launch (start us, length us, event | category | flops | bytes accessed | tf_op | source)
XLA Modules:
  0.0 49.5 jit_solution(13226919951197530335)
XLA Ops:
  1.3 45.4 %late_interaction.1 = (f32[3]{0:T(128)}, f32[1]{0:T(128)}) custom-call(bf16[3,32,768]{2,1,0:T(8,128)(2,1)} %qh.1, bf16[3,512,768]{2,1,0:T(8,128)(2,1)} %dh.1, bf16[3,4,512,768]{3,2,1,0:T(8,128)(2,1)} %nh.1, s32[3,32]{1,0:T(4,128)} %qm.1, s32[3,512]{1,0:T(4,128)} %dm.1, s32[3,4,512]{2,1,0:T(4,128)} %nm.1, f32[3,5]{1,0:T(4,128)} %te.1, bf16[768,128]{1,0:T(8,128)(2,1)} %w.1, ...), custom_call_target="tpu_custom_call" | custom-call | flops 6360662016 | bytes 11943936 | tf_op jit(solution)/shard_map/late_interaction/pallas_call | solution.py:262
  46.7 1.1 %copy.14 = f32[3]{0:T(128)} copy(f32[3]{0:T(128)} %get-tuple-element.4) | data formatting | bytes 24

commit v2 on v0

v2 whole, which is shorter than its diff:
```python
import jax
import jax.numpy as jnp
from jax import lax
from jax.experimental import pallas as pl
from jax.experimental.pallas import tpu as pltpu
from jax.sharding import PartitionSpec as P

RING = 4
CHIPS = RING ** 3
ORDERS = ((0, 1, 2), (1, 2, 0), (2, 0, 1))
SLOTS = ((0, 0), (0, 1), (0, 3), (0, 2), (1, 0), (3, 0), (2, 0), (1, 1),
         (3, 1), (2, 1), (1, 3), (3, 3), (2, 3), (1, 2), (3, 2), (2, 2))
NEAR_FIRST = (1, 3, 2)
OTHERS = sorted([(x, y, z) for x in range(RING) for y in range(RING) for z in range(RING) if x or y or z],
                key=lambda v: -sum(min(a, RING - a) for a in v))
LOW = -3.0e38
MESH = pl.DeviceIdType.MESH


def kernel(qh, dh, nh, qm, dm, nm, te, w, tau_ref, loss_ref, mean_ref,
           qv, dv, nv, qmv, dmv, nmv, tev, wv, gath, docs, best, hard, ones, dense, rest_ref, inbox, tot, totin,
           in_sem, doc_sem, gsend, grecv, osend, orecv, tsem):
    me = lax.axis_index('data')
    core = lax.rem(me, 2)
    chip = me // 2
    pos = (lax.rem(chip, RING), lax.rem(chip // RING, RING), chip // (RING * RING))
    nq, dlen, width = dv.shape
    nneg, qlen, proj = nv.shape[1], qv.shape[1], wv.shape[1]
    tau = tau_ref[0]

    def device(steps):
        c = [lax.rem(pos[a] + steps[a], RING) if steps[a] else pos[a] for a in range(3)]
        return {'data': ((c[2] * RING + c[1]) * RING + c[0]) * 2 + core}

    def along(axis, off):
        return device([off if a == axis else 0 for a in range(3)])

    partner = {'data': chip * 2 + 1 - core}

    def remote(src, dst, send, recv, target):
        return pltpu.make_async_remote_copy(src_ref=src, dst_ref=dst, send_sem=send, recv_sem=recv,
                                            device_id=target, device_id_type=MESH)

    pairs = ((w, wv), (qh, qv), (qm, qmv), (dm, dmv), (nm, nmv), (te, tev))
    loads = [pltpu.make_async_copy(src, dst, in_sem.at[n]) for n, (src, dst) in enumerate(pairs)]
    first, small = loads[:3], loads[3:]
    doc_loads = [pltpu.make_async_copy(dh.at[j], dv.at[j], in_sem.at[6 + j]) for j in range(nq)]
    neg_loads = [pltpu.make_async_copy(nh.at[i], nv.at[i], in_sem.at[6 + nq + i]) for i in range(nq)]
    for load in first + small + doc_loads + neg_loads:
        load.start()

    barrier = pltpu.get_barrier_semaphore()
    for axis in range(3):
        for off in range(1, RING):
            pl.semaphore_signal(barrier, inc=1, device_id=along(axis, off), device_id_type=MESH)
    pl.semaphore_signal(barrier, inc=1, device_id=partner, device_id_type=MESH)

    def project(rows):
        y = jnp.dot(rows, wv[...], preferred_element_type=jnp.float32)
        return y * lax.rsqrt(jnp.sum(y * y, axis=-1, keepdims=True))

    def length(mask_row):
        return jnp.sum(mask_row.astype(jnp.float32), axis=-1, keepdims=True)

    def row_ids(rows, cols):
        return lax.broadcasted_iota(jnp.int32, (rows, cols), 0).astype(jnp.float32)

    hard[...] = jnp.zeros_like(hard)
    dense[...] = jnp.zeros_like(dense)
    e_row = lax.broadcasted_iota(jnp.int32, ones.shape, 0)
    e_lane = lax.rem(lax.broadcasted_iota(jnp.int32, ones.shape, 1), RING) * qlen
    ones[...] = jnp.where((e_row >= e_lane) & (e_row < e_lane + qlen), 1.0, 0.0)

    for load in first:
        load.wait()
    for q in range(nq):
        tok = project(qv[q])
        keep = row_ids(qlen, proj) < length(qmv[q:q + 1, :])
        gath[q * RING + pos[ORDERS[q][0]]] = jnp.where(keep, tok, 0.0).astype(jnp.bfloat16)

    pl.semaphore_wait(barrier, 3 * (RING - 1) + 1)

    slot_of = {pair: n for n, pair in enumerate(SLOTS)}

    for off in NEAR_FIRST:
        for q in range(nq):
            a1 = ORDERS[q][0]
            block = gath.at[q * RING + pos[a1]]
            remote(block, block, gsend, grecv.at[0], along(a1, off)).start()

    def row_of(n, q):
        return gath.at[pl.ds((n * nq + q) * RING, RING)]

    def send_row(r, level):
        for off in NEAR_FIRST:
            back = (0, RING - off) if level == 1 else (RING - off, r)
            for q in range(nq):
                n = slot_of[back]
                remote(row_of(slot_of[(0, r)], q), row_of(n, q), gsend, grecv.at[n],
                       along(ORDERS[q][level], off)).start()

    def arrived(n):
        part = gath.at[pl.ds(n * nq * RING, nq * RING if n else nq * (RING - 1))]
        remote(part, part, gsend, grecv.at[n], partner).wait_recv()

    for load in small:
        load.wait()

    def valid_rows(y, mask_row):
        keep = row_ids(dlen, proj) < length(mask_row)
        return jnp.where(keep, y, y[0:1, :]).astype(jnp.bfloat16)

    for j in range(nq):
        doc_loads[j].wait()
        docs[core * nq + j] = valid_rows(project(dv[j]), dmv[j:j + 1, :])

    my_docs = docs.at[pl.ds(core * nq, nq)]
    their_docs = docs.at[pl.ds((1 - core) * nq, nq)]
    doc_send = remote(my_docs, my_docs, doc_sem.at[0], doc_sem.at[1], partner)
    doc_recv = remote(their_docs, their_docs, doc_sem.at[0], doc_sem.at[1], partner)
    contract = (((1,), (1,)), ((), ()))
    cell_row = lax.broadcasted_iota(jnp.int32, (8, proj), 0)
    cell_lane = lax.broadcasted_iota(jnp.int32, (8, proj), 1)
    cell = cell_row * (proj // RING) + cell_lane // RING

    def negative(i, k):
        if k == 0:
            neg_loads[i].wait()
        mine = gath[i * RING + pos[ORDERS[i][0]]]
        tok = valid_rows(project(nv[i, k]), nmv[i, k:k + 1, :])
        sim = lax.dot_general(tok, mine, contract, preferred_element_type=jnp.float32)
        score = jnp.sum(jnp.max(sim, axis=0, keepdims=True), axis=1, keepdims=True)
        hard[...] = jnp.where((cell_row == i) & (cell_lane == k + 1), score, hard[...])

    def place(q, i3, i2):
        a1, a2, a3 = ORDERS[q]
        return (q * RING + lax.rem(pos[a3] + i3, RING)) * RING + lax.rem(pos[a2] + i2, RING)

    pieces = 2 * nq
    tile = 2 * proj
    tile_row = lax.broadcasted_iota(jnp.int32, (8, tile), 0)

    def segment(s):
        rows = gath[s * pieces * RING:(s + 1) * pieces * RING].reshape(pieces * RING * qlen, proj)
        for t in range(pieces * RING * qlen // tile):
            unit = jnp.zeros((8, tile), jnp.float32)
            for j in range(2 * nq):
                sim = lax.dot_general(docs[j], rows[t * tile:(t + 1) * tile], contract,
                                      preferred_element_type=jnp.float32)
                unit = jnp.where(tile_row == j, jnp.max(sim, axis=0, keepdims=True), unit)
            best[s % 2, 2 * t] = unit[:, :proj]
            best[s % 2, 2 * t + 1] = unit[:, proj:]

    def reduce_segment(s):
        flat = best[s % 2].reshape(pieces * 8, proj)
        scores = lax.dot_general(flat, ones[...], (((1,), (0,)), ((), ())), precision=lax.Precision.HIGHEST,
                                 preferred_element_type=jnp.float32).reshape(pieces, 8, proj)
        real = lax.broadcasted_iota(jnp.int32, scores.shape, 1) < 2 * nq
        top = jnp.max(jnp.where(real, scores, LOW), axis=1, keepdims=True)
        mass = jnp.sum(jnp.where(real, jnp.exp((scores - top) / tau), 0.0), axis=1, keepdims=True)
        part = top / tau + jnp.log(mass)
        packed = dense[...]
        for p in range(pieces):
            i3, i2 = SLOTS[2 * s + p // nq]
            packed = jnp.where(cell == place(p % nq, i3, i2), part[p], packed)
        dense[...] = packed
        if s == 0:
            students = hard[...]
            for q in range(nq):
                here = (cell_row == core * nq + q) & (cell_lane == pos[ORDERS[q][0]])
                hit = jnp.sum(jnp.where(here, scores[q], 0.0), axis=0, keepdims=True)
                hit = jnp.sum(hit, axis=1, keepdims=True)
                students = jnp.where((cell_row == q) & (cell_lane == 0), hit, students)
            hard[...] = students

    def log_softmax(z):
        z = z - jnp.max(z, axis=1, keepdims=True)
        return z - jnp.log(jnp.sum(jnp.exp(z), axis=1, keepdims=True))

    def finish_rows():
        logits = hard[:nq, :nneg + 1] / tau
        teacher_log = log_softmax(tev[...])
        student_log = log_softmax(logits)
        rest = jnp.sum(jnp.exp(teacher_log) * (teacher_log - student_log), axis=1, keepdims=True) - logits[:, 0:1]
        rest_ref[...] = jnp.broadcast_to(rest, rest_ref.shape)
        rest_sum = jnp.sum(rest, axis=0, keepdims=True)
        dense[...] = jnp.where((cell_row == 1) & (cell_lane == proj - 1), rest_sum, dense[...])

    negative(0, 0)
    doc_send.start()
    for n in range(1, 6):
        negative(n // nneg, n % nneg)
    arrived(0)
    send_row(0, 1)
    send_row(0, 2)
    for n in range(6, nq * nneg):
        negative(n // nneg, n % nneg)
    doc_recv.wait_recv()
    for r in (1, 3, 2):
        arrived(slot_of[(0, r)])
        send_row(r, 2)
    for s in range(len(SLOTS) // 2):
        for n in (2 * s, 2 * s + 1):
            if SLOTS[n][0]:
                arrived(n)
        if s:
            reduce_segment(s - 1)
        if s == 2:
            finish_rows()
        segment(s)
    reduce_segment(len(SLOTS) // 2 - 1)

    inbox[chip] = dense[0:2, :]
    mine = inbox.at[chip]
    for steps in OTHERS:
        remote(mine, mine, osend, orecv, device(steps)).start()
    others = inbox.at[pl.ds(0, CHIPS - 1)]
    remote(others, others, osend, orecv, partner).wait_recv()

    parts = inbox[...]
    top = jnp.max(parts, axis=0)
    lse = top + jnp.log(jnp.sum(jnp.exp(parts - top[None]), axis=0))
    r_id = lax.broadcasted_iota(jnp.int32, (2, proj), 0)
    l_id = lax.broadcasted_iota(jnp.int32, (2, proj), 1)
    r_cell = r_id * (proj // RING) + l_id // RING
    extra = jnp.where((r_id == 1) & (l_id == proj - 1), jnp.sum(parts, axis=0), 0.0)
    total = jnp.where(r_cell < nq * RING * RING, lse, extra)
    total = jnp.sum(jnp.sum(total, axis=0, keepdims=True), axis=1, keepdims=True)
    tot[...] = jnp.broadcast_to(total, tot.shape)
    swap = remote(tot, totin, tsem.at[0], tsem.at[1], partner)
    swap.start()
    for q in range(nq):
        here = (r_cell == place(q, 0, 0)) & (lax.rem(l_id, RING) == pos[ORDERS[q][0]])
        loss_ref[q] = jnp.sum(jnp.where(here, lse, 0.0)) + jnp.sum(rest_ref[q:q + 1, 0:1])
    swap.wait()
    mean_ref[0] = jnp.sum((tot[0:1, 0:1] + totin[0:1, 0:1]) / (2 * CHIPS * nq))

    doc_send.wait_send()
    remote(others, others, osend, orecv, partner).wait_send()
    sent = gath.at[pl.ds(0, nq * (RING - 1) + (len(SLOTS) - 1) * nq * RING)]
    remote(sent, sent, gsend, grecv.at[0], partner).wait_send()


def solution(mesh):
    batch_axes = ('replica', 'data')

    def local_loss(query_hidden, doc_hidden, neg_hidden, query_mask, doc_mask, neg_mask, teacher, w_proj, temperature):
        nq, qlen, width = query_hidden.shape
        dlen, nneg = doc_hidden.shape[1], neg_hidden.shape[1]
        proj = w_proj.shape[1]
        anywhere = pl.BlockSpec(memory_space=pl.ANY)
        smem = pl.BlockSpec(memory_space=pltpu.SMEM)
        rows = nq * (qlen + dlen + nneg * dlen)
        loss, mean = pl.pallas_call(
            kernel,
            name='late_interaction',
            out_shape=(jax.ShapeDtypeStruct((nq,), jnp.float32), jax.ShapeDtypeStruct((1,), jnp.float32)),
            in_specs=[anywhere] * 8 + [smem],
            out_specs=(smem, smem),
            scratch_shapes=[
                pltpu.VMEM(query_hidden.shape, jnp.bfloat16),
                pltpu.VMEM(doc_hidden.shape, jnp.bfloat16),
                pltpu.VMEM(neg_hidden.shape, jnp.bfloat16),
                pltpu.VMEM(query_mask.shape, jnp.int32),
                pltpu.VMEM(doc_mask.shape, jnp.int32),
                pltpu.VMEM(neg_mask.shape, jnp.int32),
                pltpu.VMEM(teacher.shape, jnp.float32),
                pltpu.VMEM(w_proj.shape, jnp.bfloat16),
                pltpu.VMEM((len(SLOTS) * nq * RING, qlen, proj), jnp.bfloat16),
                pltpu.VMEM((2 * nq, dlen, proj), jnp.bfloat16),
                pltpu.VMEM((2, 2 * nq, 8, proj), jnp.float32),
                pltpu.VMEM((8, proj), jnp.float32),
                pltpu.VMEM((proj, proj), jnp.float32),
                pltpu.VMEM((8, proj), jnp.float32),
                pltpu.VMEM((nq, proj), jnp.float32),
                pltpu.VMEM((CHIPS, 2, proj), jnp.float32),
                pltpu.VMEM((1, proj), jnp.float32),
                pltpu.VMEM((1, proj), jnp.float32),
                pltpu.SemaphoreType.DMA((6 + 2 * nq,)),
                pltpu.SemaphoreType.DMA((2,)),
                pltpu.SemaphoreType.DMA,
                pltpu.SemaphoreType.DMA((len(SLOTS),)),
                pltpu.SemaphoreType.DMA,
                pltpu.SemaphoreType.DMA,
                pltpu.SemaphoreType.DMA((2,)),
            ],
            compiler_params=pltpu.CompilerParams(
                collective_id=0, has_side_effects=True, vmem_limit_bytes=60 * 1024 * 1024),
            cost_estimate=pl.CostEstimate(
                flops=2 * proj * (rows * width + CHIPS * nq * qlen * 2 * nq * dlen),
                bytes_accessed=2 * rows * width, transcendentals=rows),
        )(query_hidden, doc_hidden, neg_hidden, query_mask, doc_mask, neg_mask, teacher, w_proj,
          temperature.reshape(1))
        return loss, mean

    in_specs = (P(batch_axes, None, None), P(batch_axes, None, None), P(batch_axes, None, None, None),
                P(batch_axes, None), P(batch_axes, None), P(batch_axes, None, None), P(batch_axes, None),
                P(None, None), P())
    out_specs = (P(batch_axes), P('replica'))
    return jax.shard_map(local_loss, mesh=mesh, in_specs=in_specs, out_specs=out_specs, check_vma=False)
```

time: 226 us -> 43.2 us (0.19)
  waiting for transfers between devices: 66.3 us -> 0 us
  blocking collectives: 62.8 us -> 0 us
  matrix products: 57.3 us -> 0 us
  Pallas kernels: 0 us -> 38.9 us
  between operations: 16.7 us -> 3.05 us
  other arithmetic: 7.26 us -> 0 us
  local copies, waits for them, and re-layouts: 7.83 us -> 1.11 us
  starting transfers between devices: 5.33 us -> 0 us
    psum x1 -> x0, blocking collectives: 62.8 us -> none  [local_loss(): lax.psum(jnp.sum(loss_rows), 'data') / (local_batch * group_size)]
    dot_general x36 -> x0, matrix products: 57.3 us -> none  [the longest x32 46.2 us: token_step(): jnp.einsum('id,jsd->ijs', query_step, doc_tok, preferred_element_type=jnp...]
    all_gather x1 -> x0, waiting for transfers between devices: 55.5 us -> none  [local_loss(): lax.all_gather(jnp.transpose(query_tok, (1, 0, 2)), 'data', axis=1, tiled...]
    pallas_call x0 -> x1, Pallas kernels: none -> 38.9 us  [local_loss(): pl.pallas_call(kernel, name='late_interaction', out_shape=(jax.ShapeDtype...]
    all_to_all x1 -> x0, waiting for transfers between devices: 10.8 us -> none  [local_loss(): score_rows = lax.all_to_all(columns, 'data', 0, 1, tiled=True)]
    all_to_all x1 -> x0, starting transfers between devices: 5.3 us -> none  [local_loss(): score_rows = lax.all_to_all(columns, 'data', 0, 1, tiled=True)]
    unnamed x26 -> x1, local copies, waits for them, and re-layouts: 5.91 us -> 1.11 us
    reduce_sum x6 -> x0, other arithmetic: 2.46 us -> none  [the longest x1 1.13 us: local_loss(): jnp.sum(loss_rows)]
  transfers between devices with their start and end apart: 2 -> 0, of which waited for: 2 -> 0; matrix products, arithmetic and copies ran while one was open for 6% -> 0% of each run, Pallas kernels for 0% -> 0%
where the time goes in v2:
time: 43.2 us; the launch traced here: 43 us
  Pallas kernels  38.9 us (90%)
  between operations  3.05 us (7%)
  local copies, waits for them, and re-layouts  1.11 us (3%)
    pallas_call x1, Pallas kernels, local_loss(): pl.pallas_call(kernel, name='late_interaction', out_shape=(jax.ShapeDtype...  38.9 us
    unnamed x1, local copies, waits for them, and re-layouts  1.11 us

profile of v2, /device:TPU:1, one launch (start us, length us, event | category | flops | bytes accessed | tf_op | source)
XLA Modules:
  0.0 43.0 jit_solution(9890178429646304924)
XLA Ops:
  1.3 38.9 %late_interaction.1 = (f32[3]{0:T(128)}, f32[1]{0:T(128)}) custom-call(bf16[3,32,768]{2,1,0:T(8,128)(2,1)} %qh.1, bf16[3,512,768]{2,1,0:T(8,128)(2,1)} %dh.1, bf16[3,4,512,768]{3,2,1,0:T(8,128)(2,1)} %nh.1, s32[3,32]{1,0:T(4,128)} %qm.1, s32[3,512]{1,0:T(4,128)} %dm.1, s32[3,4,512]{2,1,0:T(4,128)} %nm.1, f32[3,5]{1,0:T(4,128)} %te.1, bf16[768,128]{1,0:T(8,128)(2,1)} %w.1, ...), custom_call_target="tpu_custom_call" | custom-call | flops 6360662016 | bytes 11943936 | tf_op jit(solution)/shard_map/late_interaction/pallas_call | solution.py:254
  40.2 1.1 %copy.14 = f32[3]{0:T(128)} copy(f32[3]{0:T(128)} %get-tuple-element.4) | data formatting | bytes 24

commit v3 on v2

--- a/solution.py
+++ b/solution.py
@@ -14,12 +14,15 @@
 OTHERS = sorted([(x, y, z) for x in range(RING) for y in range(RING) for z in range(RING) if x or y or z],
                 key=lambda v: -sum(min(a, RING - a) for a in v))
 LOW = -3.0e38
+CHUNK = 256
+EARLY = 3
+GROUPS = ((0,), (1,), (2,), (3,), (4,), (5,), (6,), (7,))
 MESH = pl.DeviceIdType.MESH
 
 
 def kernel(qh, dh, nh, qm, dm, nm, te, w, tau_ref, loss_ref, mean_ref,
-           qv, dv, nv, qmv, dmv, nmv, tev, wv, gath, docs, best, hard, ones, dense, rest_ref, inbox, tot, totin,
-           in_sem, doc_sem, gsend, grecv, osend, orecv, tsem):
+           qv, dv, nv, qmv, dmv, nmv, tev, wv, gath, docs, negs, best, hard, ones, dense, rest_ref, inbox,
+           in_sem, doc_sem, gsend, grecv, osend, orecv):
     me = lax.axis_index('data')
     core = lax.rem(me, 2)
     chip = me // 2
@@ -28,14 +31,14 @@
     nneg, qlen, proj = nv.shape[1], qv.shape[1], wv.shape[1]
     tau = tau_ref[0]
 
-    def device(steps):
+    def device(steps, other=0):
         c = [lax.rem(pos[a] + steps[a], RING) if steps[a] else pos[a] for a in range(3)]
-        return {'data': ((c[2] * RING + c[1]) * RING + c[0]) * 2 + core}
+        return {'data': ((c[2] * RING + c[1]) * RING + c[0]) * 2 + (1 - core if other else core)}
 
     def along(axis, off):
         return device([off if a == axis else 0 for a in range(3)])
 
-    partner = {'data': chip * 2 + 1 - core}
+    partner = device((0, 0, 0), 1)
 
     def remote(src, dst, send, recv, target):
         return pltpu.make_async_remote_copy(src_ref=src, dst_ref=dst, send_sem=send, recv_sem=recv,
@@ -44,9 +47,9 @@
     pairs = ((w, wv), (qh, qv), (qm, qmv), (dm, dmv), (nm, nmv), (te, tev))
     loads = [pltpu.make_async_copy(src, dst, in_sem.at[n]) for n, (src, dst) in enumerate(pairs)]
     first, small = loads[:3], loads[3:]
-    doc_loads = [pltpu.make_async_copy(dh.at[j], dv.at[j], in_sem.at[6 + j]) for j in range(nq)]
-    neg_loads = [pltpu.make_async_copy(nh.at[i], nv.at[i], in_sem.at[6 + nq + i]) for i in range(nq)]
-    for load in first + small + doc_loads + neg_loads:
+    doc_load = pltpu.make_async_copy(dh, dv, in_sem.at[6])
+    neg_loads = [pltpu.make_async_copy(nh.at[i], nv.at[i], in_sem.at[7 + i]) for i in range(nq)]
+    for load in first + small + [doc_load] + neg_loads:
         load.start()
 
     barrier = pltpu.get_barrier_semaphore()
@@ -103,16 +106,20 @@
         part = gath.at[pl.ds(n * nq * RING, nq * RING if n else nq * (RING - 1))]
         remote(part, part, gsend, grecv.at[n], partner).wait_recv()
 
-    for load in small:
+    for load in small + [doc_load]:
         load.wait()
 
-    def valid_rows(y, mask_row):
-        keep = row_ids(dlen, proj) < length(mask_row)
-        return jnp.where(keep, y, y[0:1, :]).astype(jnp.bfloat16)
+    def document(rows, mask_row, out):
+        limit = length(mask_row)
+        head = None
+        for c in range(dlen // CHUNK):
+            part = pl.ds(c * CHUNK, CHUNK)
+            y = project(rows[part, :])
+            head = y[0:1, :] if head is None else head
+            out[part, :] = jnp.where(row_ids(CHUNK, proj) + c * CHUNK < limit, y, head).astype(jnp.bfloat16)
 
     for j in range(nq):
-        doc_loads[j].wait()
-        docs[core * nq + j] = valid_rows(project(dv[j]), dmv[j:j + 1, :])
+        document(dv.at[j], dmv[j:j + 1, :], docs.at[core * nq + j])
 
     my_docs = docs.at[pl.ds(core * nq, nq)]
     their_docs = docs.at[pl.ds((1 - core) * nq, nq)]
@@ -126,11 +133,17 @@
     def negative(i, k):
         if k == 0:
             neg_loads[i].wait()
-        mine = gath[i * RING + pos[ORDERS[i][0]]]
-        tok = valid_rows(project(nv[i, k]), nmv[i, k:k + 1, :])
-        sim = lax.dot_general(tok, mine, contract, preferred_element_type=jnp.float32)
-        score = jnp.sum(jnp.max(sim, axis=0, keepdims=True), axis=1, keepdims=True)
-        hard[...] = jnp.where((cell_row == i) & (cell_lane == k + 1), score, hard[...])
+        document(nv.at[i, k], nmv[i, k:k + 1, :], negs.at[i * nneg + k])
+
+    def hard_scores():
+        found = hard[...]
+        for i in range(nq):
+            mine = gath[i * RING + pos[ORDERS[i][0]]]
+            for k in range(nneg):
+                sim = lax.dot_general(negs[i * nneg + k], mine, contract, preferred_element_type=jnp.float32)
+                score = jnp.sum(jnp.max(sim, axis=0, keepdims=True), axis=1, keepdims=True)
+                found = jnp.where((cell_row == i) & (cell_lane == k + 1), score, found)
+        hard[...] = found
 
     def place(q, i3, i2):
         a1, a2, a3 = ORDERS[q]
@@ -140,12 +153,13 @@
     tile = 2 * proj
     tile_row = lax.broadcasted_iota(jnp.int32, (8, tile), 0)
 
-    def segment(s):
-        rows = gath[s * pieces * RING:(s + 1) * pieces * RING].reshape(pieces * RING * qlen, proj)
-        for t in range(pieces * RING * qlen // tile):
+    def segment(s, tiles):
+        for t in tiles:
+            at = s * pieces * RING + 2 * t * RING
+            rows = gath[at:at + 2 * RING].reshape(tile, proj)
             unit = jnp.zeros((8, tile), jnp.float32)
             for j in range(2 * nq):
-                sim = lax.dot_general(docs[j], rows[t * tile:(t + 1) * tile], contract,
+                sim = lax.dot_general(docs[j], rows, contract,
                                       preferred_element_type=jnp.float32)
                 unit = jnp.where(tile_row == j, jnp.max(sim, axis=0, keepdims=True), unit)
             best[s % 2, 2 * t] = unit[:, :proj]
@@ -188,52 +202,58 @@
 
     negative(0, 0)
     doc_send.start()
-    for n in range(1, 6):
+    for n in range(1, EARLY):
         negative(n // nneg, n % nneg)
     arrived(0)
     send_row(0, 1)
     send_row(0, 2)
-    for n in range(6, nq * nneg):
+    for n in range(EARLY, nq * nneg):
         negative(n // nneg, n % nneg)
+    hard_scores()
     doc_recv.wait_recv()
-    for r in (1, 3, 2):
-        arrived(slot_of[(0, r)])
-        send_row(r, 2)
-    for s in range(len(SLOTS) // 2):
-        for n in (2 * s, 2 * s + 1):
+    segment(0, (0,))
+    for group in GROUPS:
+        for n in range(2 * group[0], 2 * group[-1] + 2):
             if SLOTS[n][0]:
                 arrived(n)
-        if s:
-            reduce_segment(s - 1)
-        if s == 2:
-            finish_rows()
-        segment(s)
+            elif n:
+                arrived(n)
+                send_row(SLOTS[n][1], 2)
+        for s in group:
+            if s:
+                reduce_segment(s - 1)
+            if s == 2:
+                finish_rows()
+            segment(s, (0, 1, 2) if s else (1, 2))
     reduce_segment(len(SLOTS) // 2 - 1)
 
-    inbox[chip] = dense[0:2, :]
-    mine = inbox.at[chip]
-    for steps in OTHERS:
-        remote(mine, mine, osend, orecv, device(steps)).start()
-    others = inbox.at[pl.ds(0, CHIPS - 1)]
+    here = core * CHIPS + chip
+    inbox[here] = dense[0:2, :]
+    mine = inbox.at[here]
+    for steps in OTHERS + [(0, 0, 0)]:
+        for other in (0, 1):
+            if other or any(steps):
+                remote(mine, mine, osend, orecv, device(steps, other)).start()
+    others = inbox.at[pl.ds(0, 2 * CHIPS - 1)]
     remote(others, others, osend, orecv, partner).wait_recv()
 
-    parts = inbox[...]
-    top = jnp.max(parts, axis=0)
-    lse = top + jnp.log(jnp.sum(jnp.exp(parts - top[None]), axis=0))
     r_id = lax.broadcasted_iota(jnp.int32, (2, proj), 0)
     l_id = lax.broadcasted_iota(jnp.int32, (2, proj), 1)
     r_cell = r_id * (proj // RING) + l_id // RING
-    extra = jnp.where((r_id == 1) & (l_id == proj - 1), jnp.sum(parts, axis=0), 0.0)
-    total = jnp.where(r_cell < nq * RING * RING, lse, extra)
-    total = jnp.sum(jnp.sum(total, axis=0, keepdims=True), axis=1, keepdims=True)
-    tot[...] = jnp.broadcast_to(total, tot.shape)
-    swap = remote(tot, totin, tsem.at[0], tsem.at[1], partner)
-    swap.start()
+
+    def merged(which):
+        parts = inbox[pl.ds(which * CHIPS, CHIPS)]
+        top = jnp.max(parts, axis=0)
+        lse = top + jnp.log(jnp.sum(jnp.exp(parts - top[None]), axis=0))
+        extra = jnp.where((r_id == 1) & (l_id == proj - 1), jnp.sum(parts, axis=0), 0.0)
+        return lse, jnp.where(r_cell < nq * RING * RING, lse, extra)
+
+    lse, total = merged(core)
+    total = total + merged(1 - core)[1]
+    mean_ref[0] = jnp.sum(total) / (2 * CHIPS * nq)
     for q in range(nq):
-        here = (r_cell == place(q, 0, 0)) & (lax.rem(l_id, RING) == pos[ORDERS[q][0]])
-        loss_ref[q] = jnp.sum(jnp.where(here, lse, 0.0)) + jnp.sum(rest_ref[q:q + 1, 0:1])
-    swap.wait()
-    mean_ref[0] = jnp.sum((tot[0:1, 0:1] + totin[0:1, 0:1]) / (2 * CHIPS * nq))
+        spot = (r_cell == place(q, 0, 0)) & (lax.rem(l_id, RING) == pos[ORDERS[q][0]])
+        loss_ref[q] = jnp.sum(jnp.where(spot, lse, 0.0) + jnp.where((r_id == 0) & (l_id == 0), rest_ref[q:q + 1, :], 0.0))
 
     doc_send.wait_send()
     remote(others, others, osend, orecv, partner).wait_send()
@@ -268,21 +288,19 @@
                 pltpu.VMEM(w_proj.shape, jnp.bfloat16),
                 pltpu.VMEM((len(SLOTS) * nq * RING, qlen, proj), jnp.bfloat16),
                 pltpu.VMEM((2 * nq, dlen, proj), jnp.bfloat16),
+                pltpu.VMEM((nq * nneg, dlen, proj), jnp.bfloat16),
                 pltpu.VMEM((2, 2 * nq, 8, proj), jnp.float32),
                 pltpu.VMEM((8, proj), jnp.float32),
                 pltpu.VMEM((proj, proj), jnp.float32),
                 pltpu.VMEM((8, proj), jnp.float32),
                 pltpu.VMEM((nq, proj), jnp.float32),
-                pltpu.VMEM((CHIPS, 2, proj), jnp.float32),
-                pltpu.VMEM((1, proj), jnp.float32),
-                pltpu.VMEM((1, proj), jnp.float32),
-                pltpu.SemaphoreType.DMA((6 + 2 * nq,)),
+                pltpu.VMEM((2 * CHIPS, 2, proj), jnp.float32),
+                pltpu.SemaphoreType.DMA((7 + nq,)),
                 pltpu.SemaphoreType.DMA((2,)),
                 pltpu.SemaphoreType.DMA,
                 pltpu.SemaphoreType.DMA((len(SLOTS),)),
                 pltpu.SemaphoreType.DMA,
                 pltpu.SemaphoreType.DMA,
-                pltpu.SemaphoreType.DMA((2,)),
             ],
             compiler_params=pltpu.CompilerParams(
                 collective_id=0, has_side_effects=True, vmem_limit_bytes=60 * 1024 * 1024),

time: 43.2 us -> 38.1 us (0.88)
  Pallas kernels: 38.9 us -> 33.8 us
    pallas_call x1, Pallas kernels: 38.9 us -> 33.8 us  [local_loss(): pl.pallas_call(kernel, name='late_interaction', out_shape=(jax.ShapeDtype...]
where the time goes in v3:
time: 38.1 us; the launch traced here: 38 us
  Pallas kernels  33.8 us (89%)
  between operations  3.05 us (8%)
  local copies, waits for them, and re-layouts  1.11 us (3%)
    pallas_call x1, Pallas kernels, local_loss(): pl.pallas_call(kernel, name='late_interaction', out_shape=(jax.ShapeDtype...  33.8 us
    unnamed x1, local copies, waits for them, and re-layouts  1.11 us

profile of v3, /device:TPU:1, one launch (start us, length us, event | category | flops | bytes accessed | tf_op | source)
XLA Modules:
  0.0 38.0 jit_solution(15633961233657098937)
XLA Ops:
  1.3 33.8 %late_interaction.1 = (f32[3]{0:T(128)}, f32[1]{0:T(128)}) custom-call(bf16[3,32,768]{2,1,0:T(8,128)(2,1)} %qh.1, bf16[3,512,768]{2,1,0:T(8,128)(2,1)} %dh.1, bf16[3,4,512,768]{3,2,1,0:T(8,128)(2,1)} %nh.1, s32[3,32]{1,0:T(4,128)} %qm.1, s32[3,512]{1,0:T(4,128)} %dm.1, s32[3,4,512]{2,1,0:T(4,128)} %nm.1, f32[3,5]{1,0:T(4,128)} %te.1, bf16[768,128]{1,0:T(8,128)(2,1)} %w.1, ...), custom_call_target="tpu_custom_call" | custom-call | flops 6360662016 | bytes 11943936 | tf_op jit(solution)/shard_map/late_interaction/pallas_call | solution.py:274
  35.1 1.1 %copy.14 = f32[3]{0:T(128)} copy(f32[3]{0:T(128)} %get-tuple-element.4) | data formatting | bytes 24

commit v4 on v3

--- a/solution.py
+++ b/solution.py
@@ -8,19 +8,44 @@
 RING = 4
 CHIPS = RING ** 3
 ORDERS = ((0, 1, 2), (1, 2, 0), (2, 0, 1))
-SLOTS = ((0, 0), (0, 1), (0, 3), (0, 2), (1, 0), (3, 0), (2, 0), (1, 1),
-         (3, 1), (2, 1), (1, 3), (3, 3), (2, 3), (1, 2), (3, 2), (2, 2))
 NEAR_FIRST = (1, 3, 2)
+STEPS = range(1, RING)
+QUERIES = range(len(ORDERS))
+
+
+def layout():
+    runs, blocks = {}, []
+
+    def add(name, members):
+        runs[name] = (len(blocks), len(members))
+        blocks.extend(members)
+
+    add('cross', [b for q in QUERIES for b in
+                  [(q, 0, 0, 0)] + [(q, 0, 0, c) for c in STEPS] + [(q, 0, r, 0) for r in STEPS]
+                  + [(q, p, 0, 0) for p in STEPS]])
+    for r in NEAR_FIRST:
+        add((0, r), [(q, 0, r, c) for q in QUERIES for c in STEPS])
+    for p in NEAR_FIRST:
+        add((p, 0), [b for q in QUERIES for b in
+                     [(q, p, 0, c) for c in STEPS] + [(q, p, r, 0) for r in STEPS]])
+    for p, r in ((1, 1), (3, 1), (1, 3), (3, 3), (2, 1), (2, 3), (1, 2), (3, 2), (2, 2)):
+        add((p, r), [(q, p, r, c) for q in QUERIES for c in STEPS])
+    return runs, blocks
+
+
+RUNS, BLOCKS = layout()
+CROSS = len(BLOCKS[:RUNS['cross'][1]]) // len(ORDERS)
+TILE = 8
+GROUPS = ((0, 1, 2), (3, 4, 5, 6), (7, 8, 9), (10, 11, 12), (13, 14, 15), (16, 17, 18, 19), (20, 21, 22, 23))
 OTHERS = sorted([(x, y, z) for x in range(RING) for y in range(RING) for z in range(RING) if x or y or z],
                 key=lambda v: -sum(min(a, RING - a) for a in v))
 LOW = -3.0e38
 CHUNK = 256
-EARLY = 3
-GROUPS = ((0,), (1,), (2,), (3,), (4,), (5,), (6,), (7,))
+EARLY = 8
 MESH = pl.DeviceIdType.MESH
 
 
-def kernel(qh, dh, nh, qm, dm, nm, te, w, tau_ref, loss_ref, mean_ref,
+def kernel(qh, dh, nh, qm, dm, nm, te, w, tau_ref, out_ref,
            qv, dv, nv, qmv, dmv, nmv, tev, wv, gath, docs, negs, best, hard, ones, dense, rest_ref, inbox,
            in_sem, doc_sem, gsend, grecv, osend, orecv):
     me = lax.axis_index('data')
@@ -71,40 +96,47 @@
     hard[...] = jnp.zeros_like(hard)
     dense[...] = jnp.zeros_like(dense)
     e_row = lax.broadcasted_iota(jnp.int32, ones.shape, 0)
-    e_lane = lax.rem(lax.broadcasted_iota(jnp.int32, ones.shape, 1), RING) * qlen
-    ones[...] = jnp.where((e_row >= e_lane) & (e_row < e_lane + qlen), 1.0, 0.0)
+    e_from = lax.broadcasted_iota(jnp.int32, ones.shape, 1) // proj * qlen
+    ones[...] = jnp.where((e_row >= e_from) & (e_row < e_from + qlen), 1.0, 0.0).astype(jnp.bfloat16)
 
     for load in first:
         load.wait()
     for q in range(nq):
         tok = project(qv[q])
         keep = row_ids(qlen, proj) < length(qmv[q:q + 1, :])
-        gath[q * RING + pos[ORDERS[q][0]]] = jnp.where(keep, tok, 0.0).astype(jnp.bfloat16)
+        gath[q * CROSS] = jnp.where(keep, tok, 0.0).astype(jnp.bfloat16)
 
     pl.semaphore_wait(barrier, 3 * (RING - 1) + 1)
 
-    slot_of = {pair: n for n, pair in enumerate(SLOTS)}
+    sems = {name: n for n, name in enumerate(RUNS)}
+
+    def send(first, count, name, place_at, axis, off):
+        at = RUNS[name][0] + place_at
+        remote(gath.at[pl.ds(first, count)], gath.at[pl.ds(at, count)], gsend, grecv.at[sems[name]],
+               along(axis, off)).start()
+
+    def arrived(name):
+        at, count = RUNS[name]
+        part = gath.at[pl.ds(at, count if name != 'cross' else count - nq)]
+        remote(part, part, gsend, grecv.at[sems[name]], partner).wait_recv()
 
     for off in NEAR_FIRST:
         for q in range(nq):
-            a1 = ORDERS[q][0]
-            block = gath.at[q * RING + pos[a1]]
-            remote(block, block, gsend, grecv.at[0], along(a1, off)).start()
-
-    def row_of(n, q):
-        return gath.at[pl.ds((n * nq + q) * RING, RING)]
-
-    def send_row(r, level):
+            for level in range(3):
+                send(q * CROSS, 1, 'cross', q * CROSS + level * (RING - 1) + RING - off, ORDERS[q][level], off)
+
+    def send_cross():
         for off in NEAR_FIRST:
-            back = (0, RING - off) if level == 1 else (RING - off, r)
             for q in range(nq):
-                n = slot_of[back]
-                remote(row_of(slot_of[(0, r)], q), row_of(n, q), gsend, grecv.at[n],
-                       along(ORDERS[q][level], off)).start()
-
-    def arrived(n):
-        part = gath.at[pl.ds(n * nq * RING, nq * RING if n else nq * (RING - 1))]
-        remote(part, part, gsend, grecv.at[n], partner).wait_recv()
+                send(q * CROSS + 1, 3, (0, RING - off), 3 * q, ORDERS[q][1], off)
+        for off in NEAR_FIRST:
+            for q in range(nq):
+                send(q * CROSS + 1, 6, (RING - off, 0), 6 * q, ORDERS[q][2], off)
+
+    def send_row(r):
+        for off in NEAR_FIRST:
+            for q in range(nq):
+                send(RUNS[(0, r)][0] + 3 * q, 3, (RING - off, r), 3 * q, ORDERS[q][2], off)
 
     for load in small + [doc_load]:
         load.wait()
@@ -128,7 +160,7 @@
     contract = (((1,), (1,)), ((), ()))
     cell_row = lax.broadcasted_iota(jnp.int32, (8, proj), 0)
     cell_lane = lax.broadcasted_iota(jnp.int32, (8, proj), 1)
-    cell = cell_row * (proj // RING) + cell_lane // RING
+    cell = cell_row * proj + cell_lane
 
     def negative(i, k):
         if k == 0:
@@ -138,52 +170,59 @@
     def hard_scores():
         found = hard[...]
         for i in range(nq):
-            mine = gath[i * RING + pos[ORDERS[i][0]]]
+            mine = gath[i * CROSS]
             for k in range(nneg):
                 sim = lax.dot_general(negs[i * nneg + k], mine, contract, preferred_element_type=jnp.float32)
                 score = jnp.sum(jnp.max(sim, axis=0, keepdims=True), axis=1, keepdims=True)
                 found = jnp.where((cell_row == i) & (cell_lane == k + 1), score, found)
         hard[...] = found
 
-    def place(q, i3, i2):
-        a1, a2, a3 = ORDERS[q]
-        return (q * RING + lax.rem(pos[a3] + i3, RING)) * RING + lax.rem(pos[a2] + i2, RING)
-
-    pieces = 2 * nq
-    tile = 2 * proj
+    def place(q, p, r, c):
+        index = q
+        for axis, steps in zip(reversed(ORDERS[q]), (p, r, c)):
+            index = index * RING + (lax.rem(pos[axis] + steps, RING) if steps else pos[axis])
+        return index
+
+    tile = TILE * qlen
     tile_row = lax.broadcasted_iota(jnp.int32, (8, tile), 0)
 
-    def segment(s, tiles):
-        for t in tiles:
-            at = s * pieces * RING + 2 * t * RING
-            rows = gath[at:at + 2 * RING].reshape(tile, proj)
+    def segment(g):
+        for n, t in enumerate(GROUPS[g]):
+            rows = gath[t * TILE:(t + 1) * TILE].reshape(tile, proj)
             unit = jnp.zeros((8, tile), jnp.float32)
             for j in range(2 * nq):
-                sim = lax.dot_general(docs[j], rows, contract,
-                                      preferred_element_type=jnp.float32)
+                sim = lax.dot_general(docs[j], rows, contract, preferred_element_type=jnp.float32)
                 unit = jnp.where(tile_row == j, jnp.max(sim, axis=0, keepdims=True), unit)
-            best[s % 2, 2 * t] = unit[:, :proj]
-            best[s % 2, 2 * t + 1] = unit[:, proj:]
-
-    def reduce_segment(s):
-        flat = best[s % 2].reshape(pieces * 8, proj)
-        scores = lax.dot_general(flat, ones[...], (((1,), (0,)), ((), ())), precision=lax.Precision.HIGHEST,
-                                 preferred_element_type=jnp.float32).reshape(pieces, 8, proj)
+            best[g % 2, 2 * n] = unit[:, :proj]
+            best[g % 2, 2 * n + 1] = unit[:, proj:]
+
+    def reduce_segment(g):
+        pieces = 2 * len(GROUPS[g])
+        per = proj // qlen
+        flat = best[g % 2, :pieces].reshape(pieces * 8, proj)
+        high = flat.astype(jnp.bfloat16)
+        left = flat - high.astype(jnp.float32)
+        middle = left.astype(jnp.bfloat16)
+        low = (left - middle.astype(jnp.float32)).astype(jnp.bfloat16)
+        sums = jnp.dot(jnp.concatenate([high, middle, low], axis=0), ones[...], preferred_element_type=jnp.float32)
+        size = pieces * 8
+        scores = (sums[:size] + sums[size:2 * size] + sums[2 * size:]).reshape(pieces, 8, per * proj)
         real = lax.broadcasted_iota(jnp.int32, scores.shape, 1) < 2 * nq
         top = jnp.max(jnp.where(real, scores, LOW), axis=1, keepdims=True)
         mass = jnp.sum(jnp.where(real, jnp.exp((scores - top) / tau), 0.0), axis=1, keepdims=True)
         part = top / tau + jnp.log(mass)
         packed = dense[...]
-        for p in range(pieces):
-            i3, i2 = SLOTS[2 * s + p // nq]
-            packed = jnp.where(cell == place(p % nq, i3, i2), part[p], packed)
+        first = GROUPS[g][0] * TILE
+        for b in range(pieces * per):
+            values = lax.slice(part, (b // per, 0, b % per * proj), (b // per + 1, 1, (b % per + 1) * proj))[0]
+            packed = jnp.where(cell == place(*BLOCKS[first + b]), values, packed)
         dense[...] = packed
-        if s == 0:
+        if g == 0:
             students = hard[...]
             for q in range(nq):
-                here = (cell_row == core * nq + q) & (cell_lane == pos[ORDERS[q][0]])
-                hit = jnp.sum(jnp.where(here, scores[q], 0.0), axis=0, keepdims=True)
-                hit = jnp.sum(hit, axis=1, keepdims=True)
+                b = q * CROSS
+                column = lax.slice(scores, (b // per, 0, b % per * proj), (b // per + 1, 8, (b % per + 1) * proj))[0]
+                hit = jnp.sum(jnp.where(cell_row == core * nq + q, column, 0.0), axis=0, keepdims=True)
                 students = jnp.where((cell_row == q) & (cell_lane == 0), hit, students)
             hard[...] = students
 
@@ -204,28 +243,26 @@
     doc_send.start()
     for n in range(1, EARLY):
         negative(n // nneg, n % nneg)
-    arrived(0)
-    send_row(0, 1)
-    send_row(0, 2)
+    arrived('cross')
+    send_cross()
     for n in range(EARLY, nq * nneg):
         negative(n // nneg, n % nneg)
     hard_scores()
     doc_recv.wait_recv()
-    segment(0, (0,))
-    for group in GROUPS:
-        for n in range(2 * group[0], 2 * group[-1] + 2):
-            if SLOTS[n][0]:
-                arrived(n)
-            elif n:
-                arrived(n)
-                send_row(SLOTS[n][1], 2)
-        for s in group:
-            if s:
-                reduce_segment(s - 1)
-            if s == 2:
-                finish_rows()
-            segment(s, (0, 1, 2) if s else (1, 2))
-    reduce_segment(len(SLOTS) // 2 - 1)
+    waited = {'cross'}
+    for g, group in enumerate(GROUPS):
+        for name, (at, count) in RUNS.items():
+            if at < (group[-1] + 1) * TILE and name not in waited:
+                waited.add(name)
+                arrived(name)
+                if not name[0]:
+                    send_row(name[1])
+        if g:
+            reduce_segment(g - 1)
+        if g == 2:
+            finish_rows()
+        segment(g)
+    reduce_segment(len(GROUPS) - 1)
 
     here = core * CHIPS + chip
     inbox[here] = dense[0:2, :]
@@ -239,25 +276,25 @@
 
     r_id = lax.broadcasted_iota(jnp.int32, (2, proj), 0)
     l_id = lax.broadcasted_iota(jnp.int32, (2, proj), 1)
-    r_cell = r_id * (proj // RING) + l_id // RING
+    r_cell = r_id * proj + l_id
 
     def merged(which):
         parts = inbox[pl.ds(which * CHIPS, CHIPS)]
         top = jnp.max(parts, axis=0)
         lse = top + jnp.log(jnp.sum(jnp.exp(parts - top[None]), axis=0))
         extra = jnp.where((r_id == 1) & (l_id == proj - 1), jnp.sum(parts, axis=0), 0.0)
-        return lse, jnp.where(r_cell < nq * RING * RING, lse, extra)
+        return lse, jnp.where(r_cell < nq * CHIPS, lse, extra)
 
     lse, total = merged(core)
     total = total + merged(1 - core)[1]
-    mean_ref[0] = jnp.sum(total) / (2 * CHIPS * nq)
+    out_ref[nq] = jnp.sum(total) / (2 * CHIPS * nq)
     for q in range(nq):
-        spot = (r_cell == place(q, 0, 0)) & (lax.rem(l_id, RING) == pos[ORDERS[q][0]])
-        loss_ref[q] = jnp.sum(jnp.where(spot, lse, 0.0) + jnp.where((r_id == 0) & (l_id == 0), rest_ref[q:q + 1, :], 0.0))
+        spot = r_cell == place(q, 0, 0, 0)
+        out_ref[q] = jnp.sum(jnp.where(spot, lse, 0.0) + jnp.where((r_id == 0) & (l_id == 0), rest_ref[q:q + 1, :], 0.0))
 
     doc_send.wait_send()
     remote(others, others, osend, orecv, partner).wait_send()
-    sent = gath.at[pl.ds(0, nq * (RING - 1) + (len(SLOTS) - 1) * nq * RING)]
+    sent = gath.at[pl.ds(0, len(BLOCKS) - nq)]
     remote(sent, sent, gsend, grecv.at[0], partner).wait_send()
 
 
@@ -271,12 +308,12 @@
         anywhere = pl.BlockSpec(memory_space=pl.ANY)
         smem = pl.BlockSpec(memory_space=pltpu.SMEM)
         rows = nq * (qlen + dlen + nneg * dlen)
-        loss, mean = pl.pallas_call(
+        result = pl.pallas_call(
             kernel,
             name='late_interaction',
-            out_shape=(jax.ShapeDtypeStruct((nq,), jnp.float32), jax.ShapeDtypeStruct((1,), jnp.float32)),
+            out_shape=jax.ShapeDtypeStruct((nq + 1,), jnp.float32),
             in_specs=[anywhere] * 8 + [smem],
-            out_specs=(smem, smem),
+            out_specs=smem,
             scratch_shapes=[
                 pltpu.VMEM(query_hidden.shape, jnp.bfloat16),
                 pltpu.VMEM(doc_hidden.shape, jnp.bfloat16),
@@ -286,19 +323,19 @@
                 pltpu.VMEM(neg_mask.shape, jnp.int32),
                 pltpu.VMEM(teacher.shape, jnp.float32),
                 pltpu.VMEM(w_proj.shape, jnp.bfloat16),
-                pltpu.VMEM((len(SLOTS) * nq * RING, qlen, proj), jnp.bfloat16),
+                pltpu.VMEM((len(BLOCKS), qlen, proj), jnp.bfloat16),
                 pltpu.VMEM((2 * nq, dlen, proj), jnp.bfloat16),
                 pltpu.VMEM((nq * nneg, dlen, proj), jnp.bfloat16),
-                pltpu.VMEM((2, 2 * nq, 8, proj), jnp.float32),
+                pltpu.VMEM((2, 2 * max(map(len, GROUPS)), 8, proj), jnp.float32),
                 pltpu.VMEM((8, proj), jnp.float32),
-                pltpu.VMEM((proj, proj), jnp.float32),
+                pltpu.VMEM((proj, proj // qlen * proj), jnp.bfloat16),
                 pltpu.VMEM((8, proj), jnp.float32),
                 pltpu.VMEM((nq, proj), jnp.float32),
                 pltpu.VMEM((2 * CHIPS, 2, proj), jnp.float32),
                 pltpu.SemaphoreType.DMA((7 + nq,)),
                 pltpu.SemaphoreType.DMA((2,)),
                 pltpu.SemaphoreType.DMA,
-                pltpu.SemaphoreType.DMA((len(SLOTS),)),
+                pltpu.SemaphoreType.DMA((len(RUNS),)),
                 pltpu.SemaphoreType.DMA,
                 pltpu.SemaphoreType.DMA,
             ],
@@ -309,7 +346,7 @@
                 bytes_accessed=2 * rows * width, transcendentals=rows),
         )(query_hidden, doc_hidden, neg_hidden, query_mask, doc_mask, neg_mask, teacher, w_proj,
           temperature.reshape(1))
-        return loss, mean
+        return result[:nq], result[nq:]
 
     in_specs = (P(batch_axes, None, None), P(batch_axes, None, None), P(batch_axes, None, None, None),
                 P(batch_axes, None), P(batch_axes, None), P(batch_axes, None, None), P(batch_axes, None),

time: 38.1 us -> 36.7 us (0.963)
  between operations: 3.05 us -> 1.29 us
  local copies, waits for them, and re-layouts: 1.11 us -> 2.45 us
  Pallas kernels: 33.8 us -> 32.8 us
    slice x0 -> x1, local copies, waits for them, and re-layouts: none -> 1.26 us  [local_loss(): return (result[:nq], result[nq:])]
    pallas_call x1, Pallas kernels: 33.8 us -> 32.8 us  [local_loss(): pl.pallas_call(kernel, name='late_interaction', out_shape=jax.ShapeDtypeS...]
where the time goes in v4:
time: 36.7 us; the launch traced here: 36.6 us
  Pallas kernels  32.8 us (89%)
  local copies, waits for them, and re-layouts  2.45 us (7%)
  between operations  1.29 us (4%)
    pallas_call x1, Pallas kernels, local_loss(): pl.pallas_call(kernel, name='late_interaction', out_shape=jax.ShapeDtypeS...  32.8 us
    slice x1, local copies, waits for them, and re-layouts, local_loss(): return (result[:nq], result[nq:])  1.26 us
    unnamed x1, local copies, waits for them, and re-layouts  1.19 us

profile of v4, /device:TPU:1, one launch (start us, length us, event | category | flops | bytes accessed | tf_op | source)
XLA Modules:
  0.0 36.6 jit_solution(1790623687915241244)
XLA Ops:
  1.3 32.8 %late_interaction.1 = f32[4]{0:T(128)} custom-call(bf16[3,32,768]{2,1,0:T(8,128)(2,1)} %qh.1, bf16[3,512,768]{2,1,0:T(8,128)(2,1)} %dh.1, bf16[3,4,512,768]{3,2,1,0:T(8,128)(2,1)} %nh.1, s32[3,32]{1,0:T(4,128)} %qm.1, s32[3,512]{1,0:T(4,128)} %dm.1, s32[3,4,512]{2,1,0:T(4,128)} %nm.1, f32[3,5]{1,0:T(4,128)} %te.1, bf16[768,128]{1,0:T(8,128)(2,1)} %w.1, ...), custom_call_target="tpu_custom_call" | custom-call | flops 6360662016 | bytes 11943936 | tf_op jit(solution)/shard_map/late_interaction/pallas_call | solution.py:311
  34.1 1.3 %slice.7 = f32[1]{0:T(128)} slice(f32[4]{0:T(128)} %late_interaction.1), slice={[3:4]} | slice | bytes 8 | tf_op jit(solution)/shard_map/slice | solution.py:349
  35.4 1.2 %copy.13 = f32[3]{0:T(128)} copy(f32[3]{0:T(128)} %bitcast.3) | data formatting | bytes 24

commit v5 on v4

--- a/solution.py
+++ b/solution.py
@@ -287,15 +287,23 @@
 
     lse, total = merged(core)
     total = total + merged(1 - core)[1]
-    out_ref[nq] = jnp.sum(total) / (2 * CHIPS * nq)
+    values = jnp.where((cell_row == 0) & (cell_lane == nq), jnp.sum(jnp.sum(total, axis=0, keepdims=True), axis=1, keepdims=True) / (2 * CHIPS * nq), 0.0)
     for q in range(nq):
         spot = r_cell == place(q, 0, 0, 0)
-        out_ref[q] = jnp.sum(jnp.where(spot, lse, 0.0) + jnp.where((r_id == 0) & (l_id == 0), rest_ref[q:q + 1, :], 0.0))
+        mine_q = jnp.sum(jnp.sum(jnp.where(spot, lse, 0.0), axis=0, keepdims=True), axis=1, keepdims=True) + rest_ref[q:q + 1, 0:1]
+        values = jnp.where((cell_row == 0) & (cell_lane == q), mine_q, values)
+    out_ref[...] = values
 
     doc_send.wait_send()
     remote(others, others, osend, orecv, partner).wait_send()
     sent = gath.at[pl.ds(0, len(BLOCKS) - nq)]
     remote(sent, sent, gsend, grecv.at[0], partner).wait_send()
+
+
+def split(packed, loss_ref, mean_ref):
+    for q in range(loss_ref.shape[0]):
+        loss_ref[q] = packed[0, q]
+    mean_ref[0] = packed[0, loss_ref.shape[0]]
 
 
 def solution(mesh):
@@ -311,9 +319,9 @@
         result = pl.pallas_call(
             kernel,
             name='late_interaction',
-            out_shape=jax.ShapeDtypeStruct((nq + 1,), jnp.float32),
+            out_shape=pltpu.VMEM((8, 128), jnp.float32),
             in_specs=[anywhere] * 8 + [smem],
-            out_specs=smem,
+            out_specs=pl.BlockSpec(memory_space=pltpu.VMEM),
             scratch_shapes=[
                 pltpu.VMEM(query_hidden.shape, jnp.bfloat16),
                 pltpu.VMEM(doc_hidden.shape, jnp.bfloat16),
@@ -346,7 +354,13 @@
                 bytes_accessed=2 * rows * width, transcendentals=rows),
         )(query_hidden, doc_hidden, neg_hidden, query_mask, doc_mask, neg_mask, teacher, w_proj,
           temperature.reshape(1))
-        return result[:nq], result[nq:]
+        return pl.pallas_call(
+            split,
+            name='split_results',
+            out_shape=(jax.ShapeDtypeStruct((nq,), jnp.float32), jax.ShapeDtypeStruct((1,), jnp.float32)),
+            in_specs=[pl.BlockSpec(memory_space=pltpu.VMEM)],
+            out_specs=(smem, smem),
+        )(pltpu.with_memory_space_constraint(result, pltpu.VMEM))
 
     in_specs = (P(batch_axes, None, None), P(batch_axes, None, None), P(batch_axes, None, None, None),
                 P(batch_axes, None), P(batch_axes, None), P(batch_axes, None, None), P(batch_axes, None),

time: 36.7 us -> 34.5 us (0.940)
  local copies, waits for them, and re-layouts: 2.45 us -> 0 us
    slice x1 -> x0, local copies, waits for them, and re-layouts: 1.26 us -> none  [local_loss(): return (result[:nq], result[nq:])]
    unnamed x1 -> x0, local copies, waits for them, and re-layouts: 1.19 us -> none
    pallas_call x1 -> x2, Pallas kernels: 32.8 us -> 32.9 us  [the longest x1 32.3 us: local_loss(): pl.pallas_call(kernel, name='late_interaction', out_shape=pltpu.VMEM((8,...]
where the time goes in v5:
time: 34.5 us; the launch traced here: 34.3 us
  Pallas kernels  32.9 us (95%)
  between operations  1.45 us (4%)
    pallas_call x1, Pallas kernels, local_loss(): pl.pallas_call(kernel, name='late_interaction', out_shape=pltpu.VMEM((8,...  32.3 us

profile of v5, /device:TPU:1, one launch (start us, length us, event | category | flops | bytes accessed | tf_op | source)
XLA Modules:
  0.0 34.3 jit_solution(14219370161500906896)
XLA Ops:
  1.3 32.3 %late_interaction.1.packed = f32[8,128]{1,0:T(8,128)S(1)} custom-call(bf16[3,32,768]{2,1,0:T(8,128)(2,1)} %qh.1, bf16[3,512,768]{2,1,0:T(8,128)(2,1)} %dh.1, bf16[3,4,512,768]{3,2,1,0:T(8,128)(2,1)} %nh.1, s32[3,32]{1,0:T(4,128)} %qm.1, s32[3,512]{1,0:T(4,128)} %dm.1, s32[3,4,512]{2,1,0:T(4,128)} %nm.1, f32[3,5]{1,0:T(4,128)} %te.1, bf16[768,128]{1,0:T(8,128)(2,1)} %w.1, ...), custom_call_target="tpu_custom_call" | custom-call | flops 6360662016 | bytes 11943936 | tf_op jit(solution)/shard_map/late_interaction/pallas_call | solution.py:319
  33.5 0.6 %split_results.1 = (f32[3]{0:T(128)}, f32[1]{0:T(128)}) custom-call(f32[8,128]{1,0:T(8,128)S(1)} %late_interaction.1.packed), custom_call_target="tpu_custom_call" | custom-call | tf_op jit(solution)/shard_map/split_results/pallas_call | solution.py:357

commit v6 on v5

--- a/solution.py
+++ b/solution.py
@@ -7,7 +7,7 @@
 
 RING = 4
 CHIPS = RING ** 3
-ORDERS = ((0, 1, 2), (1, 2, 0), (2, 0, 1))
+ORDERS = ((0, 2, 1), (1, 0, 2), (2, 1, 0))
 NEAR_FIRST = (1, 3, 2)
 STEPS = range(1, RING)
 QUERIES = range(len(ORDERS))
@@ -41,7 +41,7 @@
                 key=lambda v: -sum(min(a, RING - a) for a in v))
 LOW = -3.0e38
 CHUNK = 256
-EARLY = 8
+EARLY = 6
 MESH = pl.DeviceIdType.MESH
 
 
@@ -268,7 +268,7 @@
     inbox[here] = dense[0:2, :]
     mine = inbox.at[here]
     for steps in OTHERS + [(0, 0, 0)]:
-        for other in (0, 1):
+        for other in (1, 0):
             if other or any(steps):
                 remote(mine, mine, osend, orecv, device(steps, other)).start()
     others = inbox.at[pl.ds(0, 2 * CHIPS - 1)]
@@ -301,9 +301,9 @@
 
 
 def split(packed, loss_ref, mean_ref):
-    for q in range(loss_ref.shape[0]):
-        loss_ref[q] = packed[0, q]
-    mean_ref[0] = packed[0, loss_ref.shape[0]]
+    count = loss_ref.shape[0]
+    loss_ref[...] = packed[0, :count]
+    mean_ref[...] = packed[0, count:count + 1]
 
 
 def solution(mesh):
@@ -359,7 +359,7 @@
             name='split_results',
             out_shape=(jax.ShapeDtypeStruct((nq,), jnp.float32), jax.ShapeDtypeStruct((1,), jnp.float32)),
             in_specs=[pl.BlockSpec(memory_space=pltpu.VMEM)],
-            out_specs=(smem, smem),
+            out_specs=(pl.BlockSpec(memory_space=pltpu.VMEM),) * 2,
         )(pltpu.with_memory_space_constraint(result, pltpu.VMEM))
 
     in_specs = (P(batch_axes, None, None), P(batch_axes, None, None), P(batch_axes, None, None, None),

time: 34.5 us -> 34.1 us (0.988)
  no operation moved by 1% of the time
where the time goes in v6:
time: 34.1 us; the launch traced here: 34 us
  Pallas kernels  32.7 us (96%)
  between operations  1.29 us (4%)
    pallas_call x1, Pallas kernels, local_loss(): pl.pallas_call(kernel, name='late_interaction', out_shape=pltpu.VMEM((8,...  32.1 us

profile of v6, /device:TPU:1, one launch (start us, length us, event | category | flops | bytes accessed | tf_op | source)
XLA Modules:
  0.0 34.0 jit_solution(17618305086705492509)
XLA Ops:
  1.3 32.1 %late_interaction.1.packed = f32[8,128]{1,0:T(8,128)S(1)} custom-call(bf16[3,32,768]{2,1,0:T(8,128)(2,1)} %qh.1, bf16[3,512,768]{2,1,0:T(8,128)(2,1)} %dh.1, bf16[3,4,512,768]{3,2,1,0:T(8,128)(2,1)} %nh.1, s32[3,32]{1,0:T(4,128)} %qm.1, s32[3,512]{1,0:T(4,128)} %dm.1, s32[3,4,512]{2,1,0:T(4,128)} %nm.1, f32[3,5]{1,0:T(4,128)} %te.1, bf16[768,128]{1,0:T(8,128)(2,1)} %w.1, ...), custom_call_target="tpu_custom_call" | custom-call | flops 6360662016 | bytes 11943936 | tf_op jit(solution)/shard_map/late_interaction/pallas_call | solution.py:319
  33.4 0.6 %split_results.1 = (f32[3]{0:T(128)}, f32[1]{0:T(128)}) custom-call(f32[8,128]{1,0:T(8,128)S(1)} %late_interaction.1.packed), custom_call_target="tpu_custom_call" | custom-call | tf_op jit(solution)/shard_map/split_results/pallas_call | solution.py:357
